TPU v7x, 32 devices: a whole 2x2x4 slice. The times are simulated.
32 devices in a mesh: dp: 16 (over z, y, core), tp: 2 (over x).
Axes of the slice: x: 2, y: 2, z: 4, core: 2. Of those that a mesh axis runs over, the one named last changes fastest.
Arguments:
- activations: bfloat16 [2048, 2304], P('dp'), may hold values from -6 to 6
- out_grads: bfloat16 [2048, 2048], P('dp', 'tp'), may hold values from -6 to 6
- right_prev: float32 [2048, 128], P('tp'), may hold values from -6 to 6
Outputs:
- update: float32 [2304, 2048], P('dp', 'tp')
- residual: bfloat16 [36864, 2048], P('dp', 'tp')
All inputs are finite; a program needn't handle non-finite values.
Results may differ from a plain program's by a relative error of at most 0.001.
Values sent between devices are 32-bit elements; how exact they have to be, the bound alone decides.
No kernel may reach another device: no remote copies, remote signals or barrier semaphores. Data moves between devices by JAX's collectives and lax.ppermute only.
A program may use at most 64 MiB of HBM per device.

v0:
```python
import jax
import jax.numpy as jnp
from jax import lax
from jax.sharding import PartitionSpec as P


def gram_of(left_rows):
    return jnp.dot(left_rows.T, left_rows, precision=lax.Precision.HIGHEST)


def finish(left_rows, gram_matrix):
    ridge = 1e-06 * jnp.trace(gram_matrix) / gram_matrix.shape[0]
    gram_matrix = gram_matrix + ridge * jnp.eye(gram_matrix.shape[0], dtype=gram_matrix.dtype)
    lower = jnp.linalg.cholesky(gram_matrix)
    return jax.scipy.linalg.solve_triangular(lower, left_rows.T, lower=True).T


def per_device(activations, out_grads, right_prev):
    gradient = jnp.dot(activations.T, out_grads, preferred_element_type=jnp.float32)
    left_part = jnp.dot(gradient, right_prev, precision=lax.Precision.HIGHEST)
    left_sum = lax.psum(left_part, ("dp", "tp"))
    left_basis = finish(left_sum, gram_of(left_sum))
    right_part = jnp.dot(gradient.T, left_basis, precision=lax.Precision.HIGHEST)
    right_factor = lax.psum(right_part, "dp") / lax.axis_size("dp")
    update_full = jnp.dot(left_basis, right_factor.T, precision=lax.Precision.HIGHEST)
    residual = (gradient - update_full).astype(jnp.bfloat16)
    rows_dev = update_full.shape[0] // lax.axis_size("dp")
    first_row = lax.axis_index("dp") * rows_dev
    update = lax.dynamic_slice_in_dim(update_full, first_row, rows_dev, 0)
    return (update, residual)


def solution(mesh):
    in_specs = (P("dp", None), P("dp", "tp"), P("tp", None))
    out_specs = (P("dp", "tp"), P("dp", "tp"))
    return jax.shard_map(
        per_device, mesh=mesh, in_specs=in_specs, out_specs=out_specs, check_vma=False
    )
```

profile of v0, /device:TPU:0, one launch (start us, length us, event | category | flops | bytes accessed | tf_op | source)
XLA Modules:
  0.0 314.1 jit_solution(11109167322946106435)
XLA Ops:
  7.2 0.0 copy-start
  7.2 0.0 copy-start.3
  7.2 0.0 all-reduce.3.cloned.1.call-start
  7.2 1.0 copy-done
  8.2 2.4 fusion.9
  10.6 0.0 copy-start.1
  10.6 3.6 %copy-done.1 = f32[2304,1024]{1,0:T(8,128)} copy-done((f32[2304,1024]{1,0:T(8,128)}, f32[2304,1024]{1,0:T(8,128)S(1)}, u32[]{:S(2)}) %copy-start.1) | copy-done | bytes 9437208
  14.2 0.0 copy-done.3
  14.2 8.6 %fusion.10 = f32[2304,128]{1,0:T(8,128)} fusion(f32[2304,1024]{1,0:T(8,128)S(1)} %fusion.9, f32[1024,128]{1,0:T(8,128)S(1)} %copy-done.3), kind=kOutput, calls=%fused_computation.20 | convolution fusion | flops 3623878656 | bytes 11141120 | tf_op jit(solution)/shard_map/dot_general | solution.py:20
  22.8 0.0 all-reduce.3.cloned.1.call-update
  22.8 0.2 all-reduce.5.cloned.1.call-start
  23.0 134.3 %all-reduce.3.cloned.1.call-done = f32[2304,128]{1,0:T(8,128)} async-done(((f32[2304,128]{1,0:T(8,128)}), f32[2304,128]{1,0:T(8,128)}) %all-reduce.3.cloned.1.call-update) | async-done | bytes 1179664 | tf_op jit(solution)/shard_map/psum | solution.py:21
  157.4 0.0 copy-start.2
  157.4 4.3 %select_reduce_fusion.1 = (f32[]{:T(128)}, f32[128,128]{1,0:T(8,128)S(1)}) fusion(f32[2304,128]{1,0:T(8,128)} %all-reduce.3.cloned.1.call-done), kind=kOutput, calls=%fused_computation.13 | convolution fusion | flops 453033984 | bytes 1245188 | tf_op jit(solution)/shard_map/dot_general | solution.py:8
  161.7 0.1 copy.5
  162.5 11.7 %cholesky.17 = f32[128,128]{1,0:T(8,128)S(1)} custom-call(f32[128,128]{1,0:T(8,128)S(1)} %fusion.7), custom_call_target="Cholesky" | custom-call | tf_op jit(solution)/shard_map/jit(cholesky)/cholesky | solution.py:14
  174.2 0.6 compare_reduce_fusion
  174.9 0.7 fusion.3
  175.5 9.8 %custom-call.7 = f32[1,128,128]{1,2,0:T(8,128)S(1)} custom-call(f32[1,128,128]{2,1,0:T(8,128)S(1)} %fusion.3), custom_call_target="InvertDiagBlocksLowerTriangular" | custom-call | tf_op jit(solution)/shard_map/jit(_solve_triangular)/triangular_solve | solution.py:15
  185.4 0.0 copy-done.2
  185.4 1.2 fusion.4
  186.6 18.2 %fusion.11 = f32[1024,128]{1,0:T(8,128)} fusion(f32[2304,1024]{1,0:T(8,128)} %copy-done.1, f32[128,2304]{1,0:T(8,128)S(1)} %fusion.4), kind=kOutput, calls=%fused_computation.21 | convolution fusion | flops 3623878656 | bytes 11141120 | tf_op jit(solution)/shard_map/dot_general | solution.py:23
  204.8 0.0 all-reduce.5.cloned.1.call-update
  204.8 89.8 %all-reduce.5.cloned.1.call-done = f32[1024,128]{1,0:T(8,128)} async-done(((f32[1024,128]{1,0:T(8,128)}), f32[1024,128]{1,0:T(8,128)}) %all-reduce.5.cloned.1.call-update) | async-done | bytes 524304 | tf_op jit(solution)/shard_map/psum | solution.py:24
  294.6 11.8 %subtract_convert_fusion = (bf16[2304,1024]{1,0:T(8,128)(2,1)}, f32[2304,1024]{1,0:T(8,128)S(1)}) fusion(f32[2304,1024]{1,0:T(8,128)} %copy-done.1, f32[128,2304]{1,0:T(8,128)S(1)} %fusion.4, f32[1024,128]{1,0:T(8,128)} %all-reduce.5.cloned.1.call-done), kind=kOutput, calls=%fused_computation | convolution fusion | flops 3628728320 | bytes 25296896 | tf_op jit(solution)/shard_map/dot_general | solution.py:25
  306.4 0.9 constant_dynamic-slice_fusion
  (2 shorter events, 0.1 us)
Async XLA Ops:
  7.2 1.1 copy-start
  7.2 7.0 %copy-start.3 = (f32[1024,128]{1,0:T(8,128)S(1)}, f32[1024,128]{1,0:T(8,128)}, u32[]{:S(2)}) copy-start(f32[1024,128]{1,0:T(8,128)} %param.5) | copy-start | bytes 1572868
  7.2 150.2 %all-reduce.3.cloned.1.call-start = ((), (), s32[]{:S(2)}) async-start(), calls=%async_computation | async-start | bytes 2359296 | tf_op jit(solution)/shard_map/psum | solution.py:21
  10.6 3.6 %copy-start.1 = (f32[2304,1024]{1,0:T(8,128)}, f32[2304,1024]{1,0:T(8,128)S(1)}, u32[]{:S(2)}) copy-start(f32[2304,1024]{1,0:T(8,128)S(1)} %fusion.9) | copy-start | bytes 28311556
  22.8 271.8 %all-reduce.5.cloned.1.call-start = ((), (), s32[]{:S(2)}) async-start(), calls=%async_computation.1 | async-start | bytes 1048576 | tf_op jit(solution)/shard_map/psum | solution.py:24
  157.4 28.0 %copy-start.2 = (f32[2304,128]{1,0:T(8,128)S(1)}, f32[2304,128]{1,0:T(8,128)}, u32[]{:S(2)}) copy-start(f32[2304,128]{1,0:T(8,128)} %all-reduce.3.cloned.1.call-done) | copy-start | bytes 3538948
Sparse Core Ops, SparseCore 0:
  22.9 134.3 all-reduce.2
  204.9 89.6 all-reduce.4
where the time goes:
time: 314 us
  waiting for transfers between devices  224 us (71%)
  matrix products  46.5 us (15%)
  other arithmetic  22.9 us (7%)
  between operations  14.8 us (5%)
  local copies, waits for them, and re-layouts  5.59 us (2%)
    psum x1, waiting for transfers between devices, per_device(): left_sum = lax.psum(left_part, ('dp', 'tp'))  134 us
    psum x1, waiting for transfers between devices, per_device(): right_factor = lax.psum(right_part, 'dp') / lax.axis_size('dp')  89.8 us
    dot_general x1, matrix products, per_device(): jnp.dot(gradient.T, left_basis, precision=lax.Precision.HIGHEST)  18.2 us
    another operation x3, other arithmetic, finish(): lower = jnp.linalg.cholesky(gram_matrix)  12.4 us
    dot_general x1, matrix products, per_device(): jnp.dot(left_basis, right_factor.T, precision=lax.Precision.HIGHEST)  11.8 us
    another operation x2, other arithmetic, finish(): return jax.scipy.linalg.solve_triangular(lower, left_rows.T, lower=True).T  10.5 us
    dot_general x1, matrix products, per_device(): left_part = jnp.dot(gradient, right_prev, precision=lax.Precision.HIGHEST)  8.57 us
  transfers between devices with their start and end apart: 2, of which 2 were waited for; matrix products, arithmetic and copies ran while one was open for 0% of the time, Pallas kernels for 0%

commit v1 on v0

--- a/solution.py
+++ b/solution.py
@@ -21,7 +21,7 @@
     left_sum = lax.psum(left_part, ("dp", "tp"))
     left_basis = finish(left_sum, gram_of(left_sum))
     right_part = jnp.dot(gradient.T, left_basis, precision=lax.Precision.HIGHEST)
-    right_factor = lax.psum(right_part, "dp") / lax.axis_size("dp")
+    right_factor = jnp.sum(lax.all_gather(right_part, "dp"), axis=0) / lax.axis_size("dp")
     update_full = jnp.dot(left_basis, right_factor.T, precision=lax.Precision.HIGHEST)
     residual = (gradient - update_full).astype(jnp.bfloat16)
     rows_dev = update_full.shape[0] // lax.axis_size("dp")

time: 314 us -> 302 us (0.962)
  waiting for transfers between devices: 224 us -> 208 us
  other arithmetic: 22.9 us -> 26.7 us
    psum x1 -> x0, waiting for transfers between devices: 89.8 us -> none  [per_device(): right_factor = lax.psum(right_part, 'dp') / lax.axis_size('dp')]
    all_gather x0 -> x1, waiting for transfers between devices: none -> 73.4 us  [per_device(): lax.all_gather(right_part, 'dp')]
    reduce_sum x0 -> x1, other arithmetic: none -> 3.82 us  [per_device(): jnp.sum(lax.all_gather(right_part, 'dp'), axis=0) / lax.axis_size('dp')]
where the time goes in v1:
time: 302 us; the launch traced here: 301 us
  waiting for transfers between devices  208 us (69%)
  matrix products  46.4 us (15%)
  other arithmetic  26.7 us (9%)
  between operations  14.8 us (5%)
  local copies, waits for them, and re-layouts  5.59 us (2%)
    psum x1, waiting for transfers between devices, per_device(): left_sum = lax.psum(left_part, ('dp', 'tp'))  134 us
    all_gather x1, waiting for transfers between devices, per_device(): lax.all_gather(right_part, 'dp')  73.4 us
    dot_general x1, matrix products, per_device(): jnp.dot(gradient.T, left_basis, precision=lax.Precision.HIGHEST)  18.2 us
    another operation x3, other arithmetic, finish(): lower = jnp.linalg.cholesky(gram_matrix)  12.4 us
    dot_general x1, matrix products, per_device(): jnp.dot(left_basis, right_factor.T, precision=lax.Precision.HIGHEST)  11.7 us
    another operation x2, other arithmetic, finish(): return jax.scipy.linalg.solve_triangular(lower, left_rows.T, lower=True).T  10.5 us
    dot_general x1, matrix products, per_device(): left_part = jnp.dot(gradient, right_prev, precision=lax.Precision.HIGHEST)  8.57 us
  transfers between devices with their start and end apart: 2, of which 2 were waited for; matrix products, arithmetic and copies ran while one was open for 0% of the time, Pallas kernels for 0%

profile of v1, /device:TPU:0, one launch (start us, length us, event | category | flops | bytes accessed | tf_op | source)
XLA Modules:
  0.0 301.4 jit_solution(9764014253778824206)
XLA Ops:
  7.2 0.0 copy-start
  7.2 0.0 copy-start.3
  7.2 0.0 all-reduce.2.cloned.1.call-start
  7.2 1.0 copy-done
  8.2 2.4 fusion.9
  10.6 0.0 copy-start.1
  10.6 3.6 %copy-done.1 = f32[2304,1024]{1,0:T(8,128)} copy-done((f32[2304,1024]{1,0:T(8,128)}, f32[2304,1024]{1,0:T(8,128)S(1)}, u32[]{:S(2)}) %copy-start.1) | copy-done | bytes 9437208
  14.2 0.0 copy-done.3
  14.2 8.6 %fusion.10 = f32[2304,128]{1,0:T(8,128)} fusion(f32[2304,1024]{1,0:T(8,128)S(1)} %fusion.9, f32[1024,128]{1,0:T(8,128)S(1)} %copy-done.3), kind=kOutput, calls=%fused_computation.20 | convolution fusion | flops 3623878656 | bytes 11141120 | tf_op jit(solution)/shard_map/dot_general | solution.py:20
  22.8 0.0 all-reduce.2.cloned.1.call-update
  22.8 0.2 all-gather.3.cloned.1.call-start
  23.0 134.3 %all-reduce.2.cloned.1.call-done = f32[2304,128]{1,0:T(8,128)} async-done(((f32[2304,128]{1,0:T(8,128)}), f32[2304,128]{1,0:T(8,128)}) %all-reduce.2.cloned.1.call-update) | async-done | bytes 1179664 | tf_op jit(solution)/shard_map/psum | solution.py:21
  157.4 0.0 copy-start.2
  157.4 4.3 %select_reduce_fusion.1 = (f32[]{:T(128)}, f32[128,128]{1,0:T(8,128)S(1)}) fusion(f32[2304,128]{1,0:T(8,128)} %all-reduce.2.cloned.1.call-done), kind=kOutput, calls=%fused_computation.13 | convolution fusion | flops 453033984 | bytes 1245188 | tf_op jit(solution)/shard_map/dot_general | solution.py:8
  161.7 0.1 copy.5
  162.5 11.7 %cholesky.17 = f32[128,128]{1,0:T(8,128)S(1)} custom-call(f32[128,128]{1,0:T(8,128)S(1)} %fusion.7), custom_call_target="Cholesky" | custom-call | tf_op jit(solution)/shard_map/jit(cholesky)/cholesky | solution.py:14
  174.2 0.6 compare_reduce_fusion
  174.9 0.7 fusion.3
  175.5 9.8 %custom-call.7 = f32[1,128,128]{1,2,0:T(8,128)S(1)} custom-call(f32[1,128,128]{2,1,0:T(8,128)S(1)} %fusion.3), custom_call_target="InvertDiagBlocksLowerTriangular" | custom-call | tf_op jit(solution)/shard_map/jit(_solve_triangular)/triangular_solve | solution.py:15
  185.4 0.0 copy-done.2
  185.4 1.2 fusion.4
  186.6 18.2 %fusion.11 = f32[1024,128]{1,0:T(8,128)} fusion(f32[2304,1024]{1,0:T(8,128)} %copy-done.1, f32[128,2304]{1,0:T(8,128)S(1)} %fusion.4), kind=kOutput, calls=%fused_computation.21 | convolution fusion | flops 3623878656 | bytes 11141120 | tf_op jit(solution)/shard_map/dot_general | solution.py:23
  204.8 0.0 all-gather.3.cloned.1.call-update
  204.8 73.4 %all-gather.3.cloned.1.call-done = f32[16384,128]{1,0:T(8,128)} async-done(((f32[1024,128]{1,0:T(8,128)}), f32[16384,128]{1,0:T(8,128)}) %all-gather.3.cloned.1.call-update) | async-done | bytes 8388624 | tf_op jit(solution)/shard_map/all_gather | solution.py:24
  278.2 3.8 %reduce_sum.20 = f32[1024,128]{1,0:T(8,128)S(1)} reduce(f32[16,1024,128]{2,1,0:T(8,128)} %bitcast.22, f32[]{:T(128)} %constant.58.clone.1), dimensions={0}, to_apply=%region_4.5 | reduce | flops 1966080 | bytes 8912900 | tf_op jit(solution)/shard_map/reduce_sum | solution.py:24
  282.0 11.7 %subtract_convert_fusion = (bf16[2304,1024]{1,0:T(8,128)(2,1)}, f32[2304,1024]{1,0:T(8,128)S(1)}) fusion(f32[2304,1024]{1,0:T(8,128)} %copy-done.1, f32[128,2304]{1,0:T(8,128)S(1)} %fusion.4, f32[1024,128]{1,0:T(8,128)S(1)} %reduce_sum.20), kind=kOutput, calls=%fused_computation | convolution fusion | flops 3628728320 | bytes 25296896 | tf_op jit(solution)/shard_map/dot_general | solution.py:25
  293.7 0.9 constant_dynamic-slice_fusion
  (2 shorter events, 0.1 us)
Async XLA Ops:
  7.2 1.1 copy-start
  7.2 7.0 %copy-start.3 = (f32[1024,128]{1,0:T(8,128)S(1)}, f32[1024,128]{1,0:T(8,128)}, u32[]{:S(2)}) copy-start(f32[1024,128]{1,0:T(8,128)} %param.5) | copy-start | bytes 1572868
  7.2 150.2 %all-reduce.2.cloned.1.call-start = ((), (), s32[]{:S(2)}) async-start(), calls=%async_computation | async-start | bytes 2359296 | tf_op jit(solution)/shard_map/psum | solution.py:21
  10.6 3.6 %copy-start.1 = (f32[2304,1024]{1,0:T(8,128)}, f32[2304,1024]{1,0:T(8,128)S(1)}, u32[]{:S(2)}) copy-start(f32[2304,1024]{1,0:T(8,128)S(1)} %fusion.9) | copy-start | bytes 28311556
  22.8 255.4 %all-gather.3.cloned.1.call-start = ((), (), s32[]{:S(2)}) async-start(), calls=%async_computation.1 | async-start | bytes 8912896 | tf_op jit(solution)/shard_map/all_gather | solution.py:24
  157.4 28.0 %copy-start.2 = (f32[2304,128]{1,0:T(8,128)S(1)}, f32[2304,128]{1,0:T(8,128)}, u32[]{:S(2)}) copy-start(f32[2304,128]{1,0:T(8,128)} %all-reduce.2.cloned.1.call-done) | copy-start | bytes 3538948
Sparse Core Ops, SparseCore 0:
  22.9 134.3 all-reduce.1
  204.9 73.2 all-gather.2
